TPU v7x, 32 devices: a whole 2x2x4 slice. The times are simulated.
32 devices in a mesh: seq: 8 (over z, y), feat: 4 (over x, core).
Axes of the slice: x: 2, y: 2, z: 4, core: 2. Of those that a mesh axis runs over, the one named last changes fastest.
Arguments:
- hidden_in: bfloat16 [4, 2048, 2048], P(None, 'seq'), may hold values from -6 to 6
- w_query: bfloat16 [2048, 256], replicated, may hold values from -0.125 to 0.125
- w_key: bfloat16 [2048, 256], replicated, may hold values from -0.125 to 0.125
- w_value: bfloat16 [2048, 2048], P(None, 'feat'), may hold values from -0.125 to 0.125
- lengths: int32 [4], replicated, may hold values from 1024 to 2048, as said below
- owners: int32 [4], replicated, may hold values from 0 to 7
Outputs:
- mixed: bfloat16 [4, 2048, 2048], P(None, 'seq', 'feat')
- state_quad: float32 [8, 4, 16, 256, 128], P('seq', None, None, 'feat')
- state_low: float32 [8, 4, 16, 17, 128], P('seq', None, 'feat')
- norm_quad: float32 [8, 4, 16, 256], P('seq', None, None, 'feat')
- norm_low: float32 [8, 4, 16, 17], P('seq', None, 'feat')
Inputs may be any that keep to these rules, and one draw needn't show every extreme that they name: `lengths`: every prompt holds 1024 to 2048 live tokens, and some prompt holds exactly 2048. `owners`: several prompts may share a decoding device.
All inputs are finite; a program needn't handle non-finite values.
Results may differ from a plain program's by a relative error of at most 0.0085.
Values may be sent and summed in bfloat16 or wider, within the bound.
A program may use at most 256 MiB of HBM per device.

v0:
```python
import jax
import jax.numpy as jnp
from jax import lax
from jax.sharding import PartitionSpec as P

H = 16
FD = 16


NORM_FLOOR = 0.0001


def prefix(part, axis, combine, identity):
    place = lax.axis_index(axis)
    gathered = jax.tree.map(lambda a: lax.all_gather(a, axis), part)
    state = jax.tree.map(lambda a, e: jnp.zeros_like(a) + jnp.asarray(e, a.dtype), part, identity)

    def one(step, state):
        return combine(
            state, jax.tree.map(lambda a: lax.dynamic_index_in_dim(a, step, 0, False), gathered)
        )

    return lax.fori_loop(0, place, one, state)


def low_features(inputs):
    constant = jnp.ones(inputs.shape[:-1] + (1,), jnp.float32)
    return jnp.concatenate([constant, inputs * FD ** (-0.25)], axis=-1)


def quad_features(leading, inputs):
    products = leading[..., :, None] * inputs[..., None, :]
    return products.reshape(inputs.shape[:-1] + (leading.shape[-1] * inputs.shape[-1],)) * (
        2.0 * FD
    ) ** (-0.5)


def add_states(earlier_part, later_part):
    return jax.tree.map(
        lambda first_term, second_term: first_term + second_term, earlier_part, later_part
    )


def project(flat_rows, weight_cols, prompts, span, heads, width_last):
    projected = jnp.dot(flat_rows, weight_cols, preferred_element_type=jnp.float32).astype(
        jnp.bfloat16
    )
    return projected.reshape(prompts, span, heads, width_last).astype(jnp.float32)


def body(hidden_in, w_query, w_key, w_value, lengths, owners):
    highest = lax.Precision.HIGHEST
    prompts, span, width = hidden_in.shape
    n_feat = lax.axis_size("feat")
    feat_index = lax.axis_index("feat")
    seq_index = lax.axis_index("seq")
    own_heads = H // n_feat
    head_dim = width // H
    flat_rows = hidden_in.reshape(prompts * span, width)
    positions = seq_index * span + jnp.arange(span, dtype=jnp.int32)
    live_mask = (positions[None, :] < lengths[:, None]).astype(jnp.float32)
    key_mask = live_mask[:, :, None, None]
    values_own = jnp.dot(flat_rows, w_value, preferred_element_type=jnp.float32).astype(
        jnp.bfloat16
    )
    value_own = values_own.reshape(prompts, span, own_heads, head_dim).astype(jnp.float32)
    query_cols = lax.dynamic_slice_in_dim(w_query, feat_index * own_heads * FD, own_heads * FD, 1)
    key_cols = lax.dynamic_slice_in_dim(w_key, feat_index * own_heads * FD, own_heads * FD, 1)
    query_own = project(flat_rows, query_cols, prompts, span, own_heads, FD)
    key_own = project(flat_rows, key_cols, prompts, span, own_heads, FD)
    key_quad = quad_features(key_own, key_own) * key_mask
    query_quad = quad_features(query_own, query_own)
    span_quad = jnp.einsum("pchf,pchd->phfd", key_quad, value_own, precision=highest)
    norm_span = jnp.sum(key_quad, axis=1)
    key_low = low_features(key_own) * key_mask
    query_low = low_features(query_own)
    span_low = jnp.einsum("pchf,pchd->phfd", key_low, value_own, precision=highest)
    low_norm = jnp.sum(key_low, axis=1)
    empty_states = (
        jnp.zeros_like(span_quad),
        jnp.zeros_like(norm_span),
        jnp.zeros_like(span_low),
        jnp.zeros_like(low_norm),
    )
    pre_quad, pre_norm, pre_low, pre_lnorm = prefix(
        (span_quad, norm_span, span_low, low_norm), "seq", add_states, empty_states
    )
    final_quad, final_norm, final_low, final_lnorm = lax.psum(
        (span_quad, norm_span, span_low, low_norm), "seq"
    )
    num_low = jnp.einsum("pchf,phfd->pchd", query_low, pre_low, precision=highest)
    den_low = jnp.einsum("pchf,phf->pch", query_low, pre_lnorm, precision=highest)
    num_quad = jnp.einsum("pchf,phfd->pchd", query_quad, pre_quad, precision=highest)
    den_quad = jnp.einsum("pchf,phf->pch", query_quad, pre_norm, precision=highest)
    final_quad, final_norm = (
        lax.all_to_all(final_quad, "feat", split_axis=2, concat_axis=1, tiled=True),
        lax.all_to_all(final_norm, "feat", split_axis=2, concat_axis=1, tiled=True),
    )
    scores = jnp.einsum("pthf,puhf->phtu", query_own, key_own, precision=highest)
    kernel = 1.0 + scores * FD ** (-0.5) + scores * scores * (0.5 / FD)
    causal = (jnp.arange(span)[:, None] >= jnp.arange(span)[None, :]).astype(jnp.float32)
    weight = kernel * causal[None, None, :, :] * live_mask[:, None, None, :]
    num_self = jnp.einsum("phtu,puhd->pthd", weight, value_own, precision=highest)
    den_self = jnp.transpose(jnp.sum(weight, axis=3), (0, 2, 1))
    numerator = num_low + num_quad + num_self
    denominator = den_low + den_quad + den_self
    attended = numerator / denominator[..., None] * live_mask[:, :, None, None]
    squares = jnp.sum(attended * attended, axis=(2, 3))
    sum_squares = lax.psum(squares, "feat")
    scaled = attended * lax.rsqrt(sum_squares / width + NORM_FLOOR)[:, :, None, None]
    mixed = scaled.astype(jnp.bfloat16).reshape(prompts, span, own_heads * head_dim)
    owned = (owners == seq_index).astype(jnp.float32)
    state_quad = (owned[:, None, None, None] * final_quad)[None]
    state_low = (owned[:, None, None, None] * final_low)[None]
    norm_quad = (owned[:, None, None] * final_norm)[None]
    norm_low = (owned[:, None, None] * final_lnorm)[None]
    return (mixed, state_quad, state_low, norm_quad, norm_low)


def solution(mesh):
    placed = (P(None, "seq", None), P(), P(), P(None, "feat"), P(), P())
    return jax.shard_map(
        body,
        mesh=mesh,
        in_specs=placed,
        out_specs=(
            P(None, "seq", "feat"),
            P("seq", None, None, "feat", None),
            P("seq", None, "feat", None, None),
            P("seq", None, None, "feat"),
            P("seq", None, "feat", None),
        ),
        check_vma=False,
    )
```

profile of v0, /device:TPU:0, one launch (start us, length us, event | category | flops | bytes accessed | tf_op | source)
XLA Modules:
  0.0 468.9 jit_solution(4810927062687896524)
XLA Ops:
  7.2 4.2 fusion.9
  12.4 2.8 bitcast_multiply_fusion
  16.1 3.3 convolution_convert_fusion
  21.3 5.5 %fusion.36 = f32[4,4,256,128]{3,2,1,0:T(8,128)} fusion(f32[4,256,4,256]{1,3,2,0:T(8,128)} %bitcast_multiply_fusion, bf16[4,256,4,128]{1,3,2,0:T(8,128)(2,1)S(1)} %copy.62), kind=kOutput, calls=%fused_computation.68 | convolution fusion | flops 1610612736 | bytes 7340032 | tf_op jit(solution)/shard_map/pchf,pchd->phfd/dot_general | solution.py:73
  27.5 57.1 %all-reduce.2 = (f32[4,4,256]{1,0,2:T(4,128)S(1)}, f32[4,4,17]{2,1,0:T(4,128)S(1)}) all-reduce(f32[4,4,256]{1,0,2:T(4,128)S(1)} %bitcast.91, f32[4,4,17]{2,1,0:T(4,128)S(1)} %fusion.17), channel_id=1, replica_groups=mesh['seq'=8,'feat'=4] {'seq'}, use_global_device_ids=true, to_apply=%region_9.10 | all-reduce | flops 4368 | bytes 34944 | tf_op jit(solution)/shard_map/psum | solution.py:88
  85.8 3.3 all-to-all-start.1
  91.1 4.1 fusion.10
  96.1 2.6 multiply_multiply_fusion.1
  98.7 1.5 fusion.1
  100.2 3.9 fusion.2
  104.1 32.0 %all_gather.27 = f32[8,4,4,256]{3,2,1,0:T(4,128)S(1)} all-gather(f32[1,4,4,256]{3,2,1,0:T(4,128)S(1)} %all_gather.26), channel_id=1, replica_groups=mesh['seq'=8,'feat'=4] {'seq'}, dimensions={0}, use_global_device_ids=true | all-gather | bytes 147456 | tf_op jit(solution)/shard_map/all_gather | solution.py:15
  136.1 33.0 %all-gather.2 = f32[32,4,17]{2,1,0:T(4,128)S(1)} all-gather(f32[4,4,17]{2,1,0:T(4,128)S(1)} %fusion.17), channel_id=4, replica_groups=mesh['seq'=8,'feat'=4] {'seq'}, dimensions={0}, use_global_device_ids=true | all-gather | bytes 9792 | tf_op jit(solution)/shard_map/all_gather | solution.py:15
  171.9 94.8 %all-gather.6.cloned.1.call-done = f32[32,4,256,128]{3,2,1,0:T(8,128)} async-done(((f32[4,4,256,128]{3,2,1,0:T(8,128)}), f32[32,4,256,128]{3,2,1,0:T(8,128)}) %all-gather.6.cloned.1.call-update) | async-done | bytes 16777232 | tf_op jit(solution)/shard_map/all_gather | solution.py:15
  267.4 41.0 %all-gather.8.cloned.1.call-done = f32[32,4,17,128]{3,1,2,0:T(4,128)} async-done(((f32[4,4,17,128]{3,1,2,0:T(4,128)}), f32[32,4,17,128]{3,1,2,0:T(4,128)}) %all-gather.8.cloned.1.call-update) | async-done | bytes 1114128 | tf_op jit(solution)/shard_map/all_gather | solution.py:15
  309.3 3.2 fusion.15
  312.4 4.3 fusion.26
  316.7 101.8 %all-reduce.6.cloned.1.call-done = (f32[4,4,256,128]{3,2,1,0:T(8,128)}, f32[4,4,17,128]{3,2,1,0:T(8,128)}) async-done(((f32[4,4,256,128]{3,2,1,0:T(8,128)}, f32[4,4,17,128]{3,2,1,0:T(8,128)}), (f32[4,4,256,128]{3,2,1,0:T(8,128)}, f32[4,4,17,128]{3,2,1,0:T(8,128)})) %all-reduce.6.cloned.1.call-update) | async-done | bytes 2236432 | tf_op jit(solution)/shard_map/psum | solution.py:88
  418.5 4.3 copy.64
  422.8 4.4 all-to-all-start
  427.3 8.3 %multiply_reduce_fusion.1 = (f32[4,256]{1,0:T(4,128)S(1)}, f32[4,256,4,128]{1,3,2,0:T(8,128)}) fusion(f32[4,256]{1,0:T(4,128)S(1)} %compare_convert_fusion, f32[4,256,4]{1,2,0:T(4,128)S(1)} %fusion.25, f32[4,4,128,256]{3,2,1,0:T(8,128)} %fusion.2, f32[4,4,128,256]{3,2,1,0:T(8,128)} %fusion.15, f32[4,4,256,128]{3,2,1,0:T(8,128)S(1)} %get-tuple-element.62, ...), kind=kOutput, calls=%fused_computation.15 | convolution fusion | flops 1613757440 | bytes 12607488 | tf_op jit(solution)/shard_map/pchf,phfd->pchd/dot_general | solution.py:93
  435.6 18.8 %psum.35 = f32[4,256]{1,0:T(4,128)S(1)} all-reduce(f32[4,256]{1,0:T(4,128)S(1)} %get-tuple-element.123), channel_id=1, replica_groups=mesh['seq'=8,'feat'=4] {'feat'}, use_global_device_ids=true, to_apply=%region_6.7 | all-reduce | flops 1024 | bytes 8192 | tf_op jit(solution)/shard_map/psum | solution.py:109
  454.4 1.8 multiply_convert_fusion
  458.4 2.4 copy.65
  460.8 1.6 broadcast_multiply_fusion.1
  (59 shorter events, 14.9 us)
Async XLA Ops:
  7.2 8.0 %copy-start = (bf16[2048,512]{1,0:T(8,128)(2,1)S(1)}, bf16[2048,512]{1,0:T(8,128)(2,1)}, u32[]{:S(2)}) copy-start(bf16[2048,512]{1,0:T(8,128)(2,1)} %param.11) | copy-start | bytes 6291460
  7.2 4.4 copy-start.5
  7.2 259.5 %all-gather.6.cloned.1.call-start = ((), (), s32[]{:S(2)}) async-start(), calls=%async_computation.2 | async-start | bytes 18874368 | tf_op jit(solution)/shard_map/all_gather | solution.py:15
  12.4 3.7 copy-start.2
  84.6 10.7 %copy-start.6 = (s32[4]{0:T(128)S(1)}, s32[4]{0:T(128)}, u32[]{:S(2)}) copy-start(s32[4]{0:T(128)} %param.13) | copy-start | bytes 52
  85.8 83.2 %all-to-all-start.1 = ((f32[4,1,1024]{2,1,0:T(1,128)}), f32[4,1,1024]{2,1,0:T(1,128)S(1)}, u32[]{:S(2)}, u32[]{:S(2)}) async-start(f32[4,1,1024]{2,1,0:T(1,128)} %reshape.161), calls=%async_computation.1 | async-start | bytes 32768 | tf_op jit(solution)/shard_map/all_to_all | solution.py:97
  89.1 219.3 %all-gather.8.cloned.1.call-start = ((), (), s32[]{:S(2)}) async-start(), calls=%async_computation.3 | async-start | bytes 1253376 | tf_op jit(solution)/shard_map/all_gather | solution.py:15
  90.2 8.4 %copy-start.3 = (f32[4,4,17,128]{3,2,1,0:T(8,128)}, f32[4,4,17,128]{3,2,1,0:T(8,128)S(1)}, u32[]{:S(2)}) copy-start(f32[4,4,17,128]{3,2,1,0:T(8,128)S(1)} %fusion.18) | copy-start | bytes 417796
  266.6 151.9 %all-reduce.6.cloned.1.call-start = ((), (), s32[]{:S(2)}) async-start(), calls=%async_computation.4 | async-start | bytes 4587520 | tf_op jit(solution)/shard_map/psum | solution.py:88
  422.8 35.6 %all-to-all-start = ((f32[4,4,256,128]{3,1,0,2:T(4,128)}), f32[4,4,256,128]{3,1,0,2:T(4,128)}, u32[]{:S(2)}, u32[]{:S(2)}) async-start(f32[4,4,256,128]{3,1,0,2:T(4,128)} %copy.64), calls=%async_computation | async-start | bytes 4194304 | tf_op jit(solution)/shard_map/all_to_all | solution.py:96
  435.6 22.0 %copy-start.4 = (f32[4,4,17,128]{3,2,1,0:T(8,128)S(1)}, f32[4,4,17,128]{3,2,1,0:T(8,128)}, u32[]{:S(2)}) copy-start(f32[4,4,17,128]{3,2,1,0:T(8,128)} %get-tuple-element.118) | copy-start | bytes 417796
  458.4 4.0 copy-start.1
Sparse Core Ops, SparseCore 0:
  26.9 239.6 all-gather.5
  269.4 38.9 all-gather.7
  312.7 105.7 all-reduce.5
where the time goes:
time: 470 us; the launch traced here: 469 us
  waiting for transfers between devices  238 us (51%)
  blocking collectives  141 us (30%)
  matrix products  39.6 us (8%)
  local copies, waits for them, and re-layouts  15.8 us (3%)
  between operations  14 us (3%)
  other arithmetic  12 us (3%)
  starting transfers between devices  7.96 us (2%)
    all_gather x2, waiting for transfers between devices, prefix(): gathered = jax.tree.map(lambda a: lax.all_gather(a, axis), part)  136 us
    psum x1, waiting for transfers between devices, body(): lax.psum((span_quad, norm_span, span_low, low_norm), 'seq')  102 us
    all_gather x2, blocking collectives, prefix(): gathered = jax.tree.map(lambda a: lax.all_gather(a, axis), part)  65 us
    psum x1, blocking collectives, body(): lax.psum((span_quad, norm_span, span_low, low_norm), 'seq')  57.1 us
    psum x1, blocking collectives, body(): sum_squares = lax.psum(squares, 'feat')  18.8 us
  transfers between devices with their start and end apart: 5, of which 3 were waited for; matrix products, arithmetic and copies ran while one was open for 8% of the time, Pallas kernels for 0%

commit v1 on v0

v1 whole, which is shorter than its diff:
```python
import functools

import jax
import jax.numpy as jnp
from jax import lax
from jax.experimental import pallas as pl
from jax.experimental.pallas import tpu as pltpu
from jax.sharding import PartitionSpec as P

H = 16
FD = 16
NORM_FLOOR = 0.0001
LANES = 128
BF = jnp.bfloat16
F32 = jnp.float32
LIN = 128
FAR = 144
ONE = 152
LIVE_ROWS = 153

NN = (((1,), (0,)), ((), ()))
NT = (((1,), (1,)), ((), ()))
TN = (((0,), (0,)), ((), ()))


def dot(a, b, dims=NN, precision=None):
    return lax.dot_general(a, b, dims, preferred_element_type=F32, precision=precision)


def iota(shape, axis):
    return lax.broadcasted_iota(jnp.int32, shape, axis)


def features(t, rows, weights):
    diag, off, lin = weights
    tokens = t.shape[1]
    blocks = [t * t * diag if diag != 1.0 else t * t]
    scaled = t * off if off != 1.0 else t
    for o in range(1, FD // 2):
        blocks.append(scaled * pltpu.roll(t, FD - o, 0))
    blocks.append(t * lin if lin != 1.0 else t)
    blocks.append(scaled[: FD // 2] * t[FD // 2 :])
    blocks.append((iota((rows - ONE, tokens), 0) == 0).astype(F32))
    return jnp.concatenate(blocks, axis=0)


def pick_matrix(first_row, count, rows):
    r = iota((count, rows), 0) + first_row
    c = iota((count, rows), 1)
    i, j = r >> 4, r & 15
    o = (j - i) & 15
    place = jnp.where(
        o < 8, o * FD + i, jnp.where(o == 8, FAR + jnp.minimum(i, j), (FD - o) * FD + j)
    )
    return (place == c)


def kernel(cfg, len_ref, x_hbm, wq_hbm, wk_hbm, wv_hbm,
           mixed, quad_out, low_out, nq_out, nl_out,
           hid, wqk, wv, qs, ks, vs, nd, part, got, presend, pre, totsend, tot,
           zsend, zgot, tsend, sqsend, sqgot, ztsend, ztgot,
           in_sem, s1, r1, sz, rz, s2, r2, s3, r3, s4, r4, s5, r5, s6, r6):
    n, nf, npr, span, heads, rows, chunk = cfg
    me, fi = lax.axis_index("seq"), lax.axis_index("feat")
    own = heads * FD
    cpp = n // npr
    head_dim = vs.shape[2] // heads

    base = pl.multiple_of((fi * own // LANES) * LANES, LANES)
    loads = [
        pltpu.make_async_copy(wq_hbm.at[:, pl.ds(base, LANES)], wqk.at[:, pl.ds(0, LANES)], in_sem.at[npr]),
        pltpu.make_async_copy(wk_hbm.at[:, pl.ds(base, LANES)], wqk.at[:, pl.ds(LANES, LANES)], in_sem.at[npr + 1]),
        pltpu.make_async_copy(wv_hbm, wv, in_sem.at[npr + 2]),
    ]
    first = me * npr // n + 1

    def prompt_at(step):
        return lax.rem(first + step, npr)

    def hid_copy(p):
        return pltpu.make_async_copy(x_hbm.at[p], hid.at[p], in_sem.at[p])

    loads[0].start()
    loads[1].start()
    hid_copy(prompt_at(0)).start()
    loads[2].start()
    for step in range(1, npr):
        hid_copy(prompt_at(step)).start()

    barrier = pltpu.get_barrier_semaphore()

    @pl.loop(1, n)
    def _(i):
        pl.semaphore_signal(barrier, 1, device_id={"seq": lax.rem(me + i, n)}, device_id_type=pl.DeviceIdType.MESH)

    for i in range(1, nf):
        pl.semaphore_signal(barrier, 1, device_id={"feat": lax.rem(fi + i, nf)}, device_id_type=pl.DeviceIdType.MESH)
    pl.semaphore_wait(barrier, n - 1 + nf - 1)

    def to_seq(src, dst, ssem, rsem, target):
        return pltpu.make_async_remote_copy(
            src_ref=src, dst_ref=dst, send_sem=ssem, recv_sem=rsem,
            device_id={"seq": target}, device_id_type=pl.DeviceIdType.MESH)

    def to_feat(src, dst, ssem, rsem, target):
        return pltpu.make_async_remote_copy(
            src_ref=src, dst_ref=dst, send_sem=ssem, recv_sem=rsem,
            device_id={"feat": target}, device_id_type=pl.DeviceIdType.MESH)

    peer = lax.rem(me + 1, n)
    fpeer = lax.rem(fi + 1, nf)
    for load in loads:
        load.wait()

    def live_row(p):
        return ((iota((1, span), 1) + me * span) < len_ref[p]).astype(F32)

    def own_half(block):
        out = block[:, :own]
        for r in range(1, LANES // own):
            out = jnp.where(lax.rem(fi, LANES // own) == r, block[:, r * own:(r + 1) * own], out)
        return out

    zsend[...] = jnp.zeros_like(zsend)

    def project(step, _):
        p = prompt_at(step)
        hid_copy(p).wait()
        x = hid[p]
        qk = dot(x, wqk[...])
        q = own_half(qk[:, :LANES]).astype(BF)
        k = own_half(qk[:, LANES:]).astype(BF)
        qs[p] = q
        ks[p] = k
        v = dot(x, wv[...]).astype(BF)
        vs[p] = v
        kt = k.astype(F32).T
        live = live_row(p)
        sums = []
        zrow = iota(zsend.shape, 0)
        z = zsend[...]
        for h in range(heads):
            phi = (features(kt[h * FD:(h + 1) * FD], rows, (1.0, 1.0, 1.0)) * live).astype(BF)
            sums.append(dot(phi, v[:, h * head_dim:(h + 1) * head_dim]).astype(BF))
            zh = dot(jnp.ones((npr * heads, span), BF), phi, NT)
            z = jnp.where(zrow == p * heads + h, zh, z)
        zsend[...] = z
        allsums = jnp.concatenate(sums, axis=0)
        for c in range(cpp):
            target = p * cpp + c
            part[target] = allsums[c * chunk:(c + 1) * chunk]

            @pl.when(target != me)
            def _():
                to_seq(part.at[target], got.at[me], s1.at[target], r1.at[me], target).start()

            @pl.when(target == me)
            def _():
                got[me] = allsums[c * chunk:(c + 1) * chunk]
        return 0

    lax.fori_loop(0, npr, project, 0)

    zgot[me] = zsend[...]

    @pl.loop(1, n)
    def _(i):
        target = lax.rem(me + i, n)
        to_seq(zsend, zgot.at[me], sz.at[i], rz.at[me], target).start()

    def inner(p, _):
        causal = iota((span, span), 0) >= iota((span, span), 1)
        keep = jnp.where(causal, live_row(p), 0.0)
        ones = jnp.ones((span, head_dim), BF)
        for h in range(heads):
            s = dot(qs[p, :, h * FD:(h + 1) * FD], ks[p, :, h * FD:(h + 1) * FD], NT)
            w = ((1.0 + s * (FD ** -0.5 + s * (0.5 / FD))) * keep).astype(BF)
            vv = jnp.concatenate([vs[p, :, h * head_dim:(h + 1) * head_dim], ones], axis=1)
            nd[p, h] = dot(w, vv)
        return 0

    lax.fori_loop(0, npr // 2, inner, 0)

    def scan(s, acc):
        @pl.when(s != me)
        def _():
            to_seq(part.at[s], got.at[s], s1.at[s], r1.at[s], peer).wait_recv()
        presend[s] = acc.astype(BF)
        return acc + got[s].astype(F32)

    total = lax.fori_loop(0, n, scan, jnp.zeros((chunk, head_dim), F32))
    totsend[...] = total.astype(BF)
    tot[me] = total.astype(BF)
    pre[me] = presend[me]

    @pl.loop(1, n)
    def _(i):
        target = lax.rem(me + i, n)
        to_seq(presend.at[target], pre.at[me], s2.at[i], r2.at[me], target).start()

    @pl.loop(1, n)
    def _(i):
        target = lax.rem(me + i, n)
        to_seq(totsend, tot.at[me], s3.at[i], r3.at[me], target).start()

    lax.fori_loop(npr // 2, npr, inner, 0)

    zpre = jnp.zeros(zsend.shape, F32)
    ztot = jnp.zeros(zsend.shape, F32)

    def zsum(s, carry):
        zp, zt = carry

        @pl.when(s != me)
        def _():
            to_seq(zsend, zgot.at[s], sz.at[0], rz.at[s], peer).wait_recv()
        part_z = zgot[s]
        return zp + jnp.where(s < me, part_z, 0.0), zt + part_z

    zpre, ztot = lax.fori_loop(0, n, zsum, (zpre, ztot))
    ztsend[...] = ztot
    ztgot[fi] = ztot
    for i in range(1, nf):
        to_feat(ztsend, ztgot.at[fi], s6.at[i], r6.at[fi], lax.rem(fi + i, nf)).start()

    @pl.loop(1, n)
    def _(i):
        src = lax.rem(me + i, n)
        to_seq(presend.at[src], pre.at[src], s2.at[i], r2.at[src], peer).wait_recv()

    zpre_ref = zsend

    @pl.loop(1, n)
    def _(i):
        to_seq(zsend, zgot.at[me], sz.at[i], rz.at[me], peer).wait_send()

    zpre_ref[...] = zpre
    sqsend[...] = jnp.zeros_like(sqsend)
    weights = (0.5 / FD, 1.0 / FD, FD ** -0.5)

    def outer(p, _):
        qt = qs[p].astype(F32).T
        state = jnp.concatenate([pre[p * cpp + c] for c in range(cpp)], axis=0)
        live = (iota((span, 1), 0) + me * span < len_ref[p]).astype(F32)
        earlier = jnp.minimum(me * span, len_ref[p]).astype(F32)
        sq = jnp.zeros((sqsend.shape[0], span), F32)
        for h in range(heads):
            phi = features(qt[h * FD:(h + 1) * FD], rows, weights).astype(BF)
            zr = zpre_ref[pl.ds(p * heads + h, 1), :]
            zr = jnp.where(iota(zr.shape, 1) == ONE, 0.0, zr)
            zb = jnp.broadcast_to(zr, (head_dim, rows)).astype(BF)
            phit = phi.T
            num = dot(phit, state[h * rows:(h + 1) * rows]) + nd[p, h, :, :head_dim]
            den = dot(phit, zb, NT) + nd[p, h, :, head_dim:] + earlier
            att = num / den * live
            nd[p, h, :, :head_dim] = att
            sq = sq + dot(jnp.ones((sqsend.shape[0], head_dim), BF), (att * att).astype(BF), NT)
        sqsend[...] = jnp.where(iota(sq.shape, 0) == p, sq, sqsend[...])
        return 0

    lax.fori_loop(0, npr, outer, 0)

    sqgot[fi] = sqsend[...]
    for i in range(1, nf):
        to_feat(sqsend, sqgot.at[fi], s4.at[i], r4.at[fi], lax.rem(fi + i, nf)).start()

    @pl.loop(1, n)
    def _(i):
        src = lax.rem(me + i, n)
        to_seq(totsend, tot.at[src], s3.at[i], r3.at[src], peer).wait_recv()

    per = FD * FD // nf
    pick = pick_matrix(0, FD * FD, rows).astype(BF)

    def spread(p, _):
        state = jnp.concatenate([tot[p * cpp + c] for c in range(cpp)], axis=0)
        for h in range(heads):
            mine = state[h * rows:(h + 1) * rows]
            full = dot(pick, mine).astype(BF)
            for f in range(nf):
                tsend[f, p, h] = full[f * per:(f + 1) * per]
            tail = mine[LIN:].astype(F32)
            low_out[p, h] = jnp.concatenate(
                [tail[ONE - LIN:ONE - LIN + 1], tail[:FD] * FD ** -0.25], axis=0)
        return 0

    lax.fori_loop(0, npr, spread, 0)
    for i in range(1, nf):
        target = lax.rem(fi + i, nf)
        to_feat(tsend.at[target], quad_out.at[fi], s5.at[i], r5.at[fi], target).start()
    quad_out[fi] = tsend[fi]

    for i in range(1, nf):
        src = lax.rem(fi + i, nf)
        to_feat(sqsend, sqgot.at[src], s4.at[i], r4.at[src], fpeer).wait_recv()
    squares = sqgot[0]
    for f in range(1, nf):
        squares = squares + sqgot[f]
    width = nf * heads * head_dim
    mean = squares * (1.0 / width) + NORM_FLOOR
    inv = lax.rsqrt(mean)
    zsq = sqsend.shape[0]

    for p in range(npr):
        col = jnp.broadcast_to(inv[p:p + 1], (LANES, span)).T
        for h in range(heads):
            mixed[p, :, h * head_dim:(h + 1) * head_dim] = (nd[p, h, :, :head_dim] * col).astype(BF)

    for i in range(1, nf):
        src = lax.rem(fi + i, nf)
        to_feat(ztsend, ztgot.at[src], s6.at[i], r6.at[src], fpeer).wait_recv()
    own_pick = pick_matrix(fi * per, per, rows).astype(F32)
    for f in range(nf):
        nq = dot(ztgot[f], own_pick, NT, lax.Precision.HIGHEST) * (2.0 * FD) ** -0.5
        for p in range(npr):
            nq_out[p, f * heads:(f + 1) * heads] = nq[p * heads:(p + 1) * heads]
    lr, lc = iota((FD + 1, rows), 0), iota((FD + 1, rows), 1)
    low_pick = jnp.where(lr == 0, (lc == ONE).astype(F32), (lc == LIN - 1 + lr).astype(F32) * FD ** -0.25)
    nl = dot(ztgot[fi], low_pick, NT, lax.Precision.HIGHEST)
    for p in range(npr):
        nl_out[p] = nl[p * heads:(p + 1) * heads]

    for i in range(1, nf):
        src = lax.rem(fi + i, nf)
        to_feat(tsend.at[src], quad_out.at[src], s5.at[i], r5.at[src], fpeer).wait_recv()

    @pl.loop(0, n)
    def _(t):
        @pl.when(t != me)
        def _():
            to_seq(part.at[t], got.at[me], s1.at[t], r1.at[me], peer).wait_send()

    @pl.loop(1, n)
    def _(i):
        target = lax.rem(me + i, n)
        to_seq(presend.at[target], pre.at[me], s2.at[i], r2.at[me], peer).wait_send()
        to_seq(totsend, tot.at[me], s3.at[i], r3.at[me], peer).wait_send()

    for i in range(1, nf):
        to_feat(sqsend, sqgot.at[fi], s4.at[i], r4.at[fi], fpeer).wait_send()
        to_feat(tsend.at[lax.rem(fi + i, nf)], quad_out.at[fi], s5.at[i], r5.at[fi], fpeer).wait_send()
        to_feat(ztsend, ztgot.at[fi], s6.at[i], r6.at[fi], fpeer).wait_send()


def body(hidden_in, w_query, w_key, w_value, lengths, owners):
    npr, span, width = hidden_in.shape
    n, nf = lax.axis_size("seq"), lax.axis_size("feat")
    heads = H // nf
    head_dim = width // H
    step = max(n, 16)
    rows = -(-LIVE_ROWS // 8) * 8
    rows = -(-rows // step) * step if rows % step else rows
    chunk = npr * heads * rows // n
    cfg = (n, nf, npr, span, heads, rows, chunk)
    per = FD * FD // nf
    dma = pltpu.SemaphoreType.DMA
    vm = pltpu.VMEM
    ph = npr * heads
    out = pl.pallas_call(
        functools.partial(kernel, cfg),
        out_shape=(
            jax.ShapeDtypeStruct((npr, span, heads * head_dim), BF),
            jax.ShapeDtypeStruct((nf, npr, heads, per, head_dim), BF),
            jax.ShapeDtypeStruct((npr, heads, FD + 1, head_dim), F32),
            jax.ShapeDtypeStruct((npr, H, per), F32),
            jax.ShapeDtypeStruct((npr, heads, FD + 1), F32),
        ),
        in_specs=[pl.BlockSpec(memory_space=pltpu.SMEM)] + [pl.BlockSpec(memory_space=pl.ANY)] * 4,
        out_specs=[pl.BlockSpec(memory_space=pltpu.VMEM)] * 5,
        scratch_shapes=[
            vm((npr, span, width), BF),
            vm((width, 2 * LANES), BF),
            vm((width, heads * head_dim), BF),
            vm((npr, span, heads * FD), BF),
            vm((npr, span, heads * FD), BF),
            vm((npr, span, heads * head_dim), BF),
            vm((npr, heads, span, 2 * head_dim), F32),
            vm((n, chunk, head_dim), BF),
            vm((n, chunk, head_dim), BF),
            vm((n, chunk, head_dim), BF),
            vm((n, chunk, head_dim), BF),
            vm((chunk, head_dim), BF),
            vm((n, chunk, head_dim), BF),
            vm((ph, rows), F32),
            vm((n, ph, rows), F32),
            vm((nf, npr, heads, per, head_dim), BF),
            vm((8, span), F32),
            vm((nf, 8, span), F32),
            vm((ph, rows), F32),
            vm((nf, ph, rows), F32),
            dma((npr + 3,)),
            dma((n,)), dma((n,)), dma((n,)), dma((n,)),
            dma((n,)), dma((n,)), dma((n,)), dma((n,)),
            dma((nf,)), dma((nf,)), dma((nf,)), dma((nf,)), dma((nf,)), dma((nf,)),
        ],
        compiler_params=pltpu.CompilerParams(
            collective_id=0, has_side_effects=True, vmem_limit_bytes=56 * 1024 * 1024
        ),
        name="layer",
    )(lengths, hidden_in, w_query, w_key, w_value)
    mixed, quad, low, nq, nl = out
    owned = (owners == lax.axis_index("seq")).astype(F32)
    quad = jnp.transpose(quad, (1, 0, 2, 3, 4)).reshape(npr, H, per, head_dim).astype(F32)
    state_quad = (owned[:, None, None, None] * (2.0 * FD) ** -0.5 * quad)[None]
    state_low = (owned[:, None, None, None] * low)[None]
    norm_quad = (owned[:, None, None] * nq)[None]
    norm_low = (owned[:, None, None] * nl)[None]
    return (mixed, state_quad, state_low, norm_quad, norm_low)


def solution(mesh):
    placed = (P(None, "seq", None), P(), P(), P(None, "feat"), P(), P())
    return jax.shard_map(
        body,
        mesh=mesh,
        in_specs=placed,
        out_specs=(
            P(None, "seq", "feat"),
            P("seq", None, None, "feat", None),
            P("seq", None, "feat", None, None),
            P("seq", None, None, "feat"),
            P("seq", None, "feat", None),
        ),
        check_vma=False,
    )
```

time: 470 us -> 84.6 us (0.18)
  the two profiles are of different devices: /device:TPU:0 before, /device:TPU:29 now
where the time goes in v1:
time: 84.6 us; the launch traced here: 84.2 us
  Pallas kernels  73.4 us (87%)
  other arithmetic  8.23 us (10%)
  local copies, waits for them, and re-layouts  1.91 us (2%)
    pallas_call x1, Pallas kernels, body(): pl.pallas_call(functools.partial(kernel, cfg), out_shape=(jax.ShapeDtypeS...  73.4 us
    mul x2, other arithmetic, body(): owned[:, None, None, None] * (2.0 * FD) ** (-0.5) * quad  2.28 us

profile of v1, /device:TPU:29, one launch (start us, length us, event | category | flops | bytes accessed | tf_op | source)
XLA Modules:
  0.0 84.2 jit_solution(4133899322251109213)
XLA Ops:
  0.6 0.7 compare_convert_fusion
  1.3 0.7 compare_select_fusion
  2.0 73.4 %layer.1 = (bf16[4,256,512]{2,1,0:T(8,128)(2,1)}, bf16[4,4,4,64,128]{4,3,2,1,0:T(8,128)(2,1)}, f32[4,4,17,128]{3,2,1,0:T(8,128)}, f32[4,16,64]{2,1,0:T(8,128)}, f32[4,4,17]{2,1,0:T(4,128)}) custom-call(s32[4]{0:T(128)} %len_ref.1, bf16[4,256,2048]{2,1,0:T(8,128)(2,1)} %x_hbm.1, bf16[2048,256]{1,0:T(8,128)(2,1)} %wq_hbm.1, bf16[2048,256]{1,0:T(8,128)(2,1)} %wk_hbm.1, ...), custom_call_target="tpu_custom_call" | custom-call | tf_op jit(solution)/shard_map/layer/pallas_call | solution.py:359
  75.4 1.4 %multiply_bitcast_fusion.2 = f32[1,4,4,17]{3,2,1,0:T(4,128)} fusion(f32[4,4,17]{2,1,0:T(4,128)} %get-tuple-element.14, f32[4]{0:T(128)S(1)} %compare_convert_fusion), kind=kLoop, calls=%fused_computation.4 | loop fusion | flops 272 | bytes 2192 | tf_op jit(solution)/shard_map/broadcast_in_dim | solution.py:407
  76.7 1.4 %multiply_bitcast_fusion.1 = f32[1,4,16,64]{3,2,1,0:T(8,128)} fusion(f32[4,16,64]{2,1,0:T(8,128)} %get-tuple-element.13, f32[4]{0:T(128)S(1)} %compare_convert_fusion), kind=kLoop, calls=%fused_computation.3 | loop fusion | flops 4096 | bytes 32784 | tf_op jit(solution)/shard_map/broadcast_in_dim | solution.py:406
  78.2 1.0 %multiply_bitcast_fusion = f32[1,4,4,17,128]{4,3,2,1,0:T(8,128)S(1)} fusion(f32[4,4,17,128]{3,2,1,0:T(8,128)} %get-tuple-element.12, f32[4]{0:T(128)S(1)} %compare_convert_fusion), kind=kLoop, calls=%fused_computation.2 | loop fusion | flops 34816 | bytes 278544 | tf_op jit(solution)/shard_map/broadcast_in_dim | solution.py:405
  79.2 0.7 copy.13
  79.9 1.5 %convert_bitcast_fusion = f32[4,4,4,64,128]{4,3,2,0,1:T(8,128)S(1)} fusion(bf16[4,4,4,64,128]{4,3,2,1,0:T(8,128)(2,1)} %get-tuple-element.11), kind=kLoop, calls=%fused_computation | loop fusion | flops 524288 | bytes 3145728 | tf_op jit(solution)/shard_map/convert_element_type | solution.py:403
  81.4 0.2 copy.12
  81.6 0.0 copy-start
  81.6 1.6 %broadcast_multiply_fusion = f32[1,4,16,64,128]{4,3,2,1,0:T(8,128)} fusion(f32[1,4,16,64,128]{4,3,2,1,0:T(8,128)S(1)} %bitcast.9, f32[4]{0:T(128)S(1)} %compare_select_fusion), kind=kLoop, calls=%fused_computation.1 | loop fusion | flops 524288 | bytes 4194320 | tf_op jit(solution)/shard_map/mul | solution.py:404
  83.3 0.0 copy-done
  83.3 1.0 %copy.15 = bf16[4,256,512]{2,1,0:T(8,128)(2,1)} copy(bf16[4,256,512]{2,1,0:T(8,128)(2,1)S(1)} %copy-done) | data formatting | bytes 2097152
Async XLA Ops:
  81.6 1.6 %copy-start = (bf16[4,256,512]{2,1,0:T(8,128)(2,1)S(1)}, bf16[4,256,512]{2,1,0:T(8,128)(2,1)}, u32[]{:S(2)}) copy-start(bf16[4,256,512]{2,1,0:T(8,128)(2,1)} %get-tuple-element.30) | copy-start | bytes 3145732

commit v2 on v1

--- a/solution.py
+++ b/solution.py
@@ -57,13 +57,17 @@
 
 def kernel(cfg, len_ref, x_hbm, wq_hbm, wk_hbm, wv_hbm,
            mixed, quad_out, low_out, nq_out, nl_out,
-           hid, wqk, wv, qs, ks, vs, nd, part, got, presend, pre, totsend, tot,
+           hid, wqk, wv, qs, ks, vs, nd, part, mgot, bsend, got, presend, prer, fwd, pre, tot,
            zsend, zgot, tsend, sqsend, sqgot, ztsend, ztgot,
-           in_sem, s1, r1, sz, rz, s2, r2, s3, r3, s4, r4, s5, r5, s6, r6):
+           in_sem, s0, r0, s1, r1, sz, rz, s2, r2, s3, r3, s4, r4, s5, r5, s6, r6, s7, r7, s8, r8):
     n, nf, npr, span, heads, rows, chunk = cfg
     me, fi = lax.axis_index("seq"), lax.axis_index("feat")
     own = heads * FD
     cpp = n // npr
+    outer_n = n // 2
+    zo, yi = me // 2, lax.rem(me, 2)
+    mate = me + 1 - 2 * yi
+    zpeer = 2 * lax.rem(zo + 1, outer_n) + yi
     head_dim = vs.shape[2] // heads
 
     base = pl.multiple_of((fi * own // LANES) * LANES, LANES)
@@ -150,14 +154,30 @@
             target = p * cpp + c
             part[target] = allsums[c * chunk:(c + 1) * chunk]
 
-            @pl.when(target != me)
+            @pl.when(c % 2 != yi)
             def _():
-                to_seq(part.at[target], got.at[me], s1.at[target], r1.at[me], target).start()
-
-            @pl.when(target == me)
+                slot = target // 2
+                to_seq(part.at[target], mgot.at[slot], s0.at[slot], r0.at[slot], mate).start()
+
+        @pl.when(step > 0)
+        def _():
+            pair_up(prompt_at(step - 1))
+        return 0
+
+    def pair_up(p):
+        for c in range(cpp // 2):
+            slot = p * (cpp // 2) + c
+            to_seq(bsend.at[slot], mgot.at[slot], s0.at[slot], r0.at[slot], mate).wait_recv()
+            both = part[2 * slot + yi].astype(F32) + mgot[slot].astype(F32)
+            bsend[slot] = both.astype(BF)
+
+            @pl.when(slot != zo)
             def _():
-                got[me] = allsums[c * chunk:(c + 1) * chunk]
-        return 0
+                to_seq(bsend.at[slot], got.at[zo], s1.at[slot], r1.at[zo], 2 * slot + yi).start()
+
+            @pl.when(slot == zo)
+            def _():
+                got[zo] = both.astype(BF)
 
     lax.fori_loop(0, npr, project, 0)
 
@@ -179,29 +199,32 @@
             nd[p, h] = dot(w, vv)
         return 0
 
-    lax.fori_loop(0, npr // 2, inner, 0)
+    lax.fori_loop(0, 1, inner, 0)
+    pair_up(prompt_at(npr - 1))
+    lax.fori_loop(1, npr // 2, inner, 0)
 
     def scan(s, acc):
-        @pl.when(s != me)
+        @pl.when(s != zo)
         def _():
-            to_seq(part.at[s], got.at[s], s1.at[s], r1.at[s], peer).wait_recv()
+            to_seq(bsend.at[s], got.at[s], s1.at[s], r1.at[s], zpeer).wait_recv()
         presend[s] = acc.astype(BF)
         return acc + got[s].astype(F32)
 
-    total = lax.fori_loop(0, n, scan, jnp.zeros((chunk, head_dim), F32))
-    totsend[...] = total.astype(BF)
+    total = lax.fori_loop(0, outer_n, scan, jnp.zeros((chunk, head_dim), F32))
     tot[me] = total.astype(BF)
-    pre[me] = presend[me]
-
-    @pl.loop(1, n)
-    def _(i):
-        target = lax.rem(me + i, n)
-        to_seq(presend.at[target], pre.at[me], s2.at[i], r2.at[me], target).start()
-
-    @pl.loop(1, n)
-    def _(i):
-        target = lax.rem(me + i, n)
-        to_seq(totsend, tot.at[me], s3.at[i], r3.at[me], target).start()
+    prer[zo] = presend[zo]
+
+    @pl.loop(1, outer_n)
+    def _(i):
+        there = lax.rem(zo + i, outer_n)
+        to_seq(presend.at[there], prer.at[zo], s2.at[i], r2.at[zo], 2 * there + yi).start()
+
+    @pl.loop(1, outer_n)
+    def _(i):
+        there = lax.rem(zo + i, outer_n)
+        to_seq(tot.at[me], tot.at[me], s3.at[i], r3.at[zo], 2 * there + yi).start()
+
+    to_seq(tot.at[me], tot.at[me], s8.at[zo], r8.at[zo], mate).start()
 
     lax.fori_loop(npr // 2, npr, inner, 0)
 
@@ -223,10 +246,20 @@
     for i in range(1, nf):
         to_feat(ztsend, ztgot.at[fi], s6.at[i], r6.at[fi], lax.rem(fi + i, nf)).start()
 
-    @pl.loop(1, n)
-    def _(i):
-        src = lax.rem(me + i, n)
-        to_seq(presend.at[src], pre.at[src], s2.at[i], r2.at[src], peer).wait_recv()
+    @pl.loop(0, outer_n)
+    def _(i):
+        there = lax.rem(zo + i, outer_n)
+
+        @pl.when(i > 0)
+        def _():
+            to_seq(presend.at[there], prer.at[there], s2.at[i], r2.at[there], zpeer).wait_recv()
+        t = 2 * there + yi
+        before = prer[there].astype(F32)
+        mine = part[t].astype(F32)
+        theirs = mgot[there].astype(F32)
+        fwd[there] = (before + jnp.where(yi == 0, mine, 0.0)).astype(BF)
+        pre[t] = (before + jnp.where(yi == 1, theirs, 0.0)).astype(BF)
+        to_seq(fwd.at[there], pre.at[t], s7.at[there], r7.at[there], mate).start()
 
     zpre_ref = zsend
 
@@ -238,7 +271,11 @@
     sqsend[...] = jnp.zeros_like(sqsend)
     weights = (0.5 / FD, 1.0 / FD, FD ** -0.5)
 
-    def outer(p, _):
+    def outer(step, _):
+        p = lax.rem(zo * npr // outer_n + step, npr)
+        for c in range(cpp // 2):
+            slot = p * (cpp // 2) + c
+            to_seq(fwd.at[slot], pre.at[2 * slot + 1 - yi], s7.at[slot], r7.at[slot], mate).wait_recv()
         qt = qs[p].astype(F32).T
         state = jnp.concatenate([pre[p * cpp + c] for c in range(cpp)], axis=0)
         live = (iota((span, 1), 0) + me * span < len_ref[p]).astype(F32)
@@ -256,6 +293,14 @@
             nd[p, h, :, :head_dim] = att
             sq = sq + dot(jnp.ones((sqsend.shape[0], head_dim), BF), (att * att).astype(BF), NT)
         sqsend[...] = jnp.where(iota(sq.shape, 0) == p, sq, sqsend[...])
+        for c in range(cpp // 2):
+            slot = p * (cpp // 2) + c
+
+            @pl.when(slot != zo)
+            def _():
+                t = 2 * slot + yi
+                to_seq(tot.at[t], tot.at[t], s3.at[slot], r3.at[slot], zpeer).wait_recv()
+                to_seq(tot.at[t], tot.at[t], s8.at[slot], r8.at[slot], mate).start()
         return 0
 
     lax.fori_loop(0, npr, outer, 0)
@@ -264,15 +309,15 @@
     for i in range(1, nf):
         to_feat(sqsend, sqgot.at[fi], s4.at[i], r4.at[fi], lax.rem(fi + i, nf)).start()
 
-    @pl.loop(1, n)
-    def _(i):
-        src = lax.rem(me + i, n)
-        to_seq(totsend, tot.at[src], s3.at[i], r3.at[src], peer).wait_recv()
-
     per = FD * FD // nf
     pick = pick_matrix(0, FD * FD, rows).astype(BF)
 
-    def spread(p, _):
+    def spread(step, _):
+        p = lax.rem(zo * npr // outer_n + step, npr)
+        for c in range(cpp // 2):
+            slot = p * (cpp // 2) + c
+            t = 2 * slot + 1 - yi
+            to_seq(tot.at[t], tot.at[t], s8.at[slot], r8.at[slot], mate).wait_recv()
         state = jnp.concatenate([tot[p * cpp + c] for c in range(cpp)], axis=0)
         for h in range(heads):
             mine = state[h * rows:(h + 1) * rows]
@@ -282,12 +327,12 @@
             tail = mine[LIN:].astype(F32)
             low_out[p, h] = jnp.concatenate(
                 [tail[ONE - LIN:ONE - LIN + 1], tail[:FD] * FD ** -0.25], axis=0)
+        for i in range(1, nf):
+            target = lax.rem(fi + i, nf)
+            to_feat(tsend.at[target, p], quad_out.at[fi, p], s5.at[i, p], r5.at[fi, p], target).start()
         return 0
 
     lax.fori_loop(0, npr, spread, 0)
-    for i in range(1, nf):
-        target = lax.rem(fi + i, nf)
-        to_feat(tsend.at[target], quad_out.at[fi], s5.at[i], r5.at[fi], target).start()
     quad_out[fi] = tsend[fi]
 
     for i in range(1, nf):
@@ -322,24 +367,42 @@
 
     for i in range(1, nf):
         src = lax.rem(fi + i, nf)
-        to_feat(tsend.at[src], quad_out.at[src], s5.at[i], r5.at[src], fpeer).wait_recv()
-
-    @pl.loop(0, n)
-    def _(t):
-        @pl.when(t != me)
+
+        @pl.loop(0, npr)
+        def _(p):
+            to_feat(tsend.at[src, p], quad_out.at[src, p], s5.at[i, p], r5.at[src, p], fpeer).wait_recv()
+            to_feat(tsend.at[src, p], quad_out.at[src, p], s5.at[i, p], r5.at[src, p], fpeer).wait_send()
+        to_feat(sqsend, sqgot.at[fi], s4.at[i], r4.at[fi], fpeer).wait_send()
+        to_feat(ztsend, ztgot.at[fi], s6.at[i], r6.at[fi], fpeer).wait_send()
+
+    @pl.loop(0, outer_n)
+    def _(slot):
+        t = 2 * slot + yi
+        to_seq(part.at[t], mgot.at[slot], s0.at[slot], r0.at[slot], mate).wait_send()
+        to_seq(fwd.at[slot], pre.at[t], s7.at[slot], r7.at[slot], mate).wait_send()
+        to_seq(tot.at[t], tot.at[t], s8.at[slot], r8.at[slot], mate).wait_send()
+
+        @pl.when(slot != zo)
         def _():
-            to_seq(part.at[t], got.at[me], s1.at[t], r1.at[me], peer).wait_send()
-
-    @pl.loop(1, n)
-    def _(i):
-        target = lax.rem(me + i, n)
-        to_seq(presend.at[target], pre.at[me], s2.at[i], r2.at[me], peer).wait_send()
-        to_seq(totsend, tot.at[me], s3.at[i], r3.at[me], peer).wait_send()
-
-    for i in range(1, nf):
-        to_feat(sqsend, sqgot.at[fi], s4.at[i], r4.at[fi], fpeer).wait_send()
-        to_feat(tsend.at[lax.rem(fi + i, nf)], quad_out.at[fi], s5.at[i], r5.at[fi], fpeer).wait_send()
-        to_feat(ztsend, ztgot.at[fi], s6.at[i], r6.at[fi], fpeer).wait_send()
+            to_seq(bsend.at[slot], got.at[zo], s1.at[slot], r1.at[zo], zpeer).wait_send()
+
+    @pl.loop(1, outer_n)
+    def _(i):
+        to_seq(presend.at[i], prer.at[zo], s2.at[i], r2.at[zo], zpeer).wait_send()
+        to_seq(tot.at[me], tot.at[me], s3.at[i], r3.at[zo], zpeer).wait_send()
+
+
+def finish(cfg, own_ref, mixed, quad, low, nq, nl, mixed_out, quad_out, low_out, nq_out, nl_out):
+    nf, heads = cfg
+    p = pl.program_id(0)
+    mask = (own_ref[p] == lax.axis_index("seq")).astype(F32)
+    mixed_out[...] = mixed[...]
+    for f in range(nf):
+        quad_out[0, f * heads:(f + 1) * heads] = quad[f, 0].astype(F32) * (mask * (2.0 * FD) ** -0.5)
+    for h in range(heads):
+        low_out[0, :, h, :] = low[0, h] * mask
+    nq_out[...] = nq[...] * mask
+    nl_out[...] = nl[...] * mask
 
 
 def body(hidden_in, w_query, w_key, w_value, lengths, owners):
@@ -376,10 +439,13 @@
             vm((npr, span, heads * head_dim), BF),
             vm((npr, heads, span, 2 * head_dim), F32),
             vm((n, chunk, head_dim), BF),
+            vm((n // 2, chunk, head_dim), BF),
+            vm((n // 2, chunk, head_dim), BF),
+            vm((n // 2, chunk, head_dim), BF),
+            vm((n // 2, chunk, head_dim), BF),
+            vm((n // 2, chunk, head_dim), BF),
+            vm((n // 2, chunk, head_dim), BF),
             vm((n, chunk, head_dim), BF),
-            vm((n, chunk, head_dim), BF),
-            vm((n, chunk, head_dim), BF),
-            vm((chunk, head_dim), BF),
             vm((n, chunk, head_dim), BF),
             vm((ph, rows), F32),
             vm((n, ph, rows), F32),
@@ -389,9 +455,10 @@
             vm((ph, rows), F32),
             vm((nf, ph, rows), F32),
             dma((npr + 3,)),
-            dma((n,)), dma((n,)), dma((n,)), dma((n,)),
-            dma((n,)), dma((n,)), dma((n,)), dma((n,)),
-            dma((nf,)), dma((nf,)), dma((nf,)), dma((nf,)), dma((nf,)), dma((nf,)),
+            dma((n // 2,)), dma((n // 2,)), dma((n // 2,)), dma((n // 2,)), dma((n,)), dma((n,)),
+            dma((n // 2,)), dma((n // 2,)), dma((n // 2,)), dma((n // 2,)),
+            dma((nf,)), dma((nf,)), dma((nf, npr)), dma((nf, npr)), dma((nf,)), dma((nf,)),
+            dma((n // 2,)), dma((n // 2,)), dma((n // 2,)), dma((n // 2,)),
         ],
         compiler_params=pltpu.CompilerParams(
             collective_id=0, has_side_effects=True, vmem_limit_bytes=56 * 1024 * 1024
@@ -399,13 +466,35 @@
         name="layer",
     )(lengths, hidden_in, w_query, w_key, w_value)
     mixed, quad, low, nq, nl = out
-    owned = (owners == lax.axis_index("seq")).astype(F32)
-    quad = jnp.transpose(quad, (1, 0, 2, 3, 4)).reshape(npr, H, per, head_dim).astype(F32)
-    state_quad = (owned[:, None, None, None] * (2.0 * FD) ** -0.5 * quad)[None]
-    state_low = (owned[:, None, None, None] * low)[None]
-    norm_quad = (owned[:, None, None] * nq)[None]
-    norm_low = (owned[:, None, None] * nl)[None]
-    return (mixed, state_quad, state_low, norm_quad, norm_low)
+    block = pl.BlockSpec
+    mixed, quad, low, nq, nl = pl.pallas_call(
+        functools.partial(finish, (nf, heads)),
+        grid=(npr,),
+        out_shape=(
+            jax.ShapeDtypeStruct(mixed.shape, BF),
+            jax.ShapeDtypeStruct((npr, H, per, head_dim), F32),
+            jax.ShapeDtypeStruct((npr, FD + 1, heads, head_dim), F32),
+            jax.ShapeDtypeStruct(nq.shape, F32),
+            jax.ShapeDtypeStruct(nl.shape, F32),
+        ),
+        in_specs=[
+            block(memory_space=pltpu.SMEM),
+            block((1, span, heads * head_dim), lambda p: (p, 0, 0)),
+            block((nf, 1, heads, per, head_dim), lambda p: (0, p, 0, 0, 0)),
+            block((1, heads, FD + 1, head_dim), lambda p: (p, 0, 0, 0)),
+            block((1, H, per), lambda p: (p, 0, 0)),
+            block((1, heads, FD + 1), lambda p: (p, 0, 0)),
+        ],
+        out_specs=[
+            block((1, span, heads * head_dim), lambda p: (p, 0, 0)),
+            block((1, H, per, head_dim), lambda p: (p, 0, 0, 0)),
+            block((1, FD + 1, heads, head_dim), lambda p: (p, 0, 0, 0)),
+            block((1, H, per), lambda p: (p, 0, 0)),
+            block((1, heads, FD + 1), lambda p: (p, 0, 0)),
+        ],
+        name="finish",
+    )(owners, mixed, quad, low, nq, nl)
+    return (mixed, quad[None], jnp.transpose(low, (0, 2, 1, 3))[None], nq[None], nl[None])
 
 
 def solution(mesh):

time: 84.6 us -> 58.6 us (0.69)
  the two profiles are of different devices: /device:TPU:29 before, /device:TPU:9 now
where the time goes in v2:
time: 58.6 us; the launch traced here: 58.4 us
  Pallas kernels  57.8 us (99%)
  between operations  0.64 us (1%)
    pallas_call x1, Pallas kernels, body(): pl.pallas_call(functools.partial(kernel, cfg), out_shape=(jax.ShapeDtypeS...  53.8 us
    pallas_call x1, Pallas kernels, body(): pl.pallas_call(functools.partial(finish, (nf, heads)), grid=(npr,), out_s...  4.01 us

profile of v2, /device:TPU:9, one launch (start us, length us, event | category | flops | bytes accessed | tf_op | source)
XLA Modules:
  0.0 58.4 jit_solution(16911523004175979455)
XLA Ops:
  0.6 53.8 %layer.1 = (bf16[4,256,512]{2,1,0:T(8,128)(2,1)}, bf16[4,4,4,64,128]{4,3,2,1,0:T(8,128)(2,1)}, f32[4,4,17,128]{3,2,1,0:T(8,128)}, f32[4,16,64]{2,1,0:T(8,128)}, f32[4,4,17]{2,1,0:T(4,128)}) custom-call(s32[4]{0:T(128)} %len_ref.1, bf16[4,256,2048]{2,1,0:T(8,128)(2,1)} %x_hbm.1, bf16[2048,256]{1,0:T(8,128)(2,1)} %wq_hbm.1, bf16[2048,256]{1,0:T(8,128)(2,1)} %wk_hbm.1, ...), custom_call_target="tpu_custom_call" | custom-call | tf_op jit(solution)/shard_map/layer/pallas_call | solution.py:422
  54.4 4.0 %finish.1 = (bf16[4,256,512]{2,1,0:T(8,128)(2,1)}, f32[4,16,64,128]{3,2,1,0:T(8,128)}, f32[4,17,4,128]{3,2,1,0:T(4,128)}, f32[4,16,64]{2,1,0:T(8,128)}, f32[4,4,17]{2,1,0:T(4,128)}) custom-call(s32[4]{0:T(128)} %own_ref.1, bf16[4,256,512]{2,1,0:T(8,128)(2,1)} %get-tuple-element.15.mixed, bf16[4,4,4,64,128]{4,3,2,1,0:T(8,128)(2,1)} %get-tuple-element.16.quad, ...), custom_call_target="tpu_custom_call" | custom-call | tf_op jit(solution)/shard_map/finish/pallas_call | solution.py:470

commit v3 on v2

v3 whole, which is shorter than its diff:
```python
import functools

import jax
import jax.numpy as jnp
from jax import lax
from jax.experimental import pallas as pl
from jax.experimental.pallas import tpu as pltpu
from jax.sharding import PartitionSpec as P

H = 16
FD = 16
NORM_FLOOR = 0.0001
LANES = 128
BF = jnp.bfloat16
F32 = jnp.float32
LIN = 128
FAR = 144
ONE = 152
LIVE_ROWS = 153

NN = (((1,), (0,)), ((), ()))
NT = (((1,), (1,)), ((), ()))
TN = (((0,), (0,)), ((), ()))


def dot(a, b, dims=NN, precision=None):
    return lax.dot_general(a, b, dims, preferred_element_type=F32, precision=precision)


def iota(shape, axis):
    return lax.broadcasted_iota(jnp.int32, shape, axis)


def features(t, rows, weights):
    diag, off, lin = weights
    tokens = t.shape[1]
    blocks = [t * t * diag if diag != 1.0 else t * t]
    scaled = t * off if off != 1.0 else t
    for o in range(1, FD // 2):
        blocks.append(scaled * pltpu.roll(t, FD - o, 0))
    blocks.append(t * lin if lin != 1.0 else t)
    blocks.append(scaled[: FD // 2] * t[FD // 2 :])
    blocks.append((iota((rows - ONE, tokens), 0) == 0).astype(F32))
    return jnp.concatenate(blocks, axis=0)


def pick_matrix(first_row, count, rows):
    r = iota((count, rows), 0) + first_row
    c = iota((count, rows), 1)
    i, j = r >> 4, r & 15
    o = (j - i) & 15
    place = jnp.where(
        o < 8, o * FD + i, jnp.where(o == 8, FAR + jnp.minimum(i, j), (FD - o) * FD + j)
    )
    return (place == c)


def kernel(cfg, len_ref, x_hbm, wq_hbm, wk_hbm, wv_hbm,
           mixed, quad_out, low_out, nq_out, nl_out,
           hid, wqk, wv, qs, ks, vs, nd, part, mgot, bsend, got, presend, prer, fwd, pre, tot,
           tsend, sqsend, sqgot, ztsend, ztgot,
           in_sem, s0, r0, s1, r1, s2, r2, s3, r3, s4, r4, s5, r5, s6, r6, s7, r7, s8, r8):
    n, nf, npr, span, heads, rows, sub = cfg
    me, fi = lax.axis_index("seq"), lax.axis_index("feat")
    own = heads * FD
    outer_n = n // 2
    zo, yi = me // 2, lax.rem(me, 2)
    mate = me + 1 - 2 * yi
    zpeer = 2 * lax.rem(zo + 1, outer_n) + yi
    head_dim = vs.shape[2] // heads

    base = pl.multiple_of((fi * own // LANES) * LANES, LANES)
    loads = [
        pltpu.make_async_copy(wq_hbm.at[:, pl.ds(base, LANES)], wqk.at[:, pl.ds(0, LANES)], in_sem.at[npr]),
        pltpu.make_async_copy(wk_hbm.at[:, pl.ds(base, LANES)], wqk.at[:, pl.ds(LANES, LANES)], in_sem.at[npr + 1]),
        pltpu.make_async_copy(wv_hbm, wv, in_sem.at[npr + 2]),
    ]
    last = outer_n - 1

    def hid_copy(p):
        return pltpu.make_async_copy(x_hbm.at[p], hid.at[p], in_sem.at[p])

    loads[0].start()
    loads[1].start()
    hid_copy(0).start()
    loads[2].start()
    for step in range(1, npr):
        hid_copy(step).start()

    barrier = pltpu.get_barrier_semaphore()

    @pl.loop(1, n)
    def _(i):
        pl.semaphore_signal(barrier, 1, device_id={"seq": lax.rem(me + i, n)}, device_id_type=pl.DeviceIdType.MESH)

    for i in range(1, nf):
        pl.semaphore_signal(barrier, 1, device_id={"feat": lax.rem(fi + i, nf)}, device_id_type=pl.DeviceIdType.MESH)
    pl.semaphore_wait(barrier, n - 1 + nf - 1)

    def to_seq(src, dst, ssem, rsem, target):
        return pltpu.make_async_remote_copy(
            src_ref=src, dst_ref=dst, send_sem=ssem, recv_sem=rsem,
            device_id={"seq": target}, device_id_type=pl.DeviceIdType.MESH)

    def to_feat(src, dst, ssem, rsem, target):
        return pltpu.make_async_remote_copy(
            src_ref=src, dst_ref=dst, send_sem=ssem, recv_sem=rsem,
            device_id={"feat": target}, device_id_type=pl.DeviceIdType.MESH)

    peer = lax.rem(me + 1, n)
    fpeer = lax.rem(fi + 1, nf)
    for load in loads:
        load.wait()

    def live_row(p):
        return ((iota((1, span), 1) + me * span) < len_ref[p]).astype(F32)

    def own_half(block):
        out = block[:, :own]
        for r in range(1, LANES // own):
            out = jnp.where(lax.rem(fi, LANES // own) == r, block[:, r * own:(r + 1) * own], out)
        return out

    def project(p, _):
        hid_copy(p).wait()
        x = hid[p]
        qk = dot(x, wqk[...])
        q = own_half(qk[:, :LANES]).astype(BF)
        k = own_half(qk[:, LANES:]).astype(BF)
        qs[p] = q
        ks[p] = k
        v = dot(x, wv[...]).astype(BF)
        vs[p] = v
        kt = k.astype(F32).T
        live = live_row(p)
        sums = []
        tail = rows - ONE
        row = iota((tail, LANES), 0)
        ones = jnp.ones((tail, span), BF)
        gap = jnp.zeros((tail, 2 * LANES - ONE - 8), F32)
        for h in range(heads):
            phi = (features(kt[h * FD:(h + 1) * FD], rows, (1.0, 1.0, 1.0)) * live).astype(BF)
            summed = dot(phi, v[:, h * head_dim:(h + 1) * head_dim])
            zh = dot(ones, phi, NT)
            more = jnp.concatenate([zh[:, LANES:ONE + 8], gap], axis=1)
            end = summed[ONE:] + jnp.where(row == 1, zh[:, :LANES], 0.0) + jnp.where(row == 2, more, 0.0)
            sums.append(jnp.concatenate([summed[:ONE], end], axis=0).astype(BF))
        half = heads // 2
        for c in range(2):
            part[p, c] = jnp.concatenate(sums[c * half:(c + 1) * half], axis=0).reshape(outer_n, sub, head_dim)
        to_seq(part.at[p, 1 - yi], mgot.at[p], s0.at[p], r0.at[p], mate).start()

        @pl.when(p > 1)
        def _():
            pair_up(p - 2)
        return 0

    def pair_up(p):
        to_seq(bsend.at[p], mgot.at[p], s0.at[p], r0.at[p], mate).wait_recv()
        bsend[p] = (part[p, yi].astype(F32) + mgot[p].astype(F32)).astype(BF)
        got[p, zo] = bsend[p, zo]

        @pl.loop(1, outer_n)
        def _(i):
            there = lax.rem(zo + i, outer_n)
            to_seq(bsend.at[p, there], got.at[p, zo], s1.at[p, i], r1.at[p, zo], 2 * there + yi).start()

    def home(p):
        def scan(z, acc):
            @pl.when(z != zo)
            def _():
                to_seq(bsend.at[p, z], got.at[p, z], s1.at[p, z], r1.at[p, z], zpeer).wait_recv()
            presend[p, z] = acc.astype(BF)
            return acc + got[p, z].astype(F32)

        total = lax.fori_loop(0, outer_n, scan, jnp.zeros((sub, head_dim), F32))
        tot[p, yi, zo] = total.astype(BF)
        prer[p, zo] = presend[p, zo]

        @pl.loop(1, outer_n)
        def _(i):
            there = lax.rem(zo + i, outer_n)

            @pl.when(there != 0)
            def _():
                to_seq(presend.at[p, there], prer.at[p, zo], s2.at[p, i], r2.at[p, zo], 2 * there + yi).start()

        @pl.loop(1, outer_n)
        def _(i):
            there = lax.rem(zo + i, outer_n)

            @pl.when(there != last)
            def _():
                to_seq(tot.at[p, yi, zo], tot.at[p, yi, zo], s3.at[p, i], r3.at[p, zo], 2 * there + yi).start()

    def take_prefix(p):
        @pl.when(zo != 0)
        def _():
            @pl.loop(1, outer_n)
            def _(i):
                there = lax.rem(zo + i, outer_n)
                to_seq(presend.at[p, there], prer.at[p, there], s2.at[p, i], r2.at[p, there], zpeer).wait_recv()

        @pl.when(zo == 0)
        def _():
            prer[p] = jnp.zeros(prer.shape[1:], BF)
        before = prer[p].astype(F32)
        fwd[p] = (before + jnp.where(yi == 0, part[p, yi].astype(F32), 0.0)).astype(BF)
        to_seq(fwd.at[p], pre.at[p, yi], s7.at[p], r7.at[p], mate).start()
        pre[p, yi] = (before + jnp.where(yi == 1, mgot[p].astype(F32), 0.0)).astype(BF)

    def take_total(p):
        @pl.when(zo != last)
        def _():
            @pl.loop(1, outer_n)
            def _(i):
                there = lax.rem(zo + i, outer_n)
                to_seq(presend.at[p, there], tot.at[p, yi, there], s3.at[p, i], r3.at[p, there], zpeer).wait_recv()
            to_seq(tot.at[p, yi], tot.at[p, yi], s8.at[p], r8.at[p], mate).start()

        @pl.when(zo == last)
        def _():
            @pl.loop(1, outer_n)
            def _(i):
                there = lax.rem(zo + i, outer_n)
                tot[p, yi, there] = (prer[p, there].astype(F32) + bsend[p, there].astype(F32)).astype(BF)
            to_seq(tot.at[p, yi], tot.at[p, yi], s8.at[p], r8.at[p], mate).start()

    lax.fori_loop(0, npr, project, 0)

    def inner(p, _):
        causal = iota((span, span), 0) >= iota((span, span), 1)
        keep = jnp.where(causal, live_row(p), 0.0)
        ones = jnp.ones((span, head_dim), BF)
        for h in range(heads):
            s = dot(qs[p, :, h * FD:(h + 1) * FD], ks[p, :, h * FD:(h + 1) * FD], NT)
            w = ((1.0 + s * (FD ** -0.5 + s * (0.5 / FD))) * keep).astype(BF)
            vv = jnp.concatenate([vs[p, :, h * head_dim:(h + 1) * head_dim], ones], axis=1)
            nd[p, h] = dot(w, vv)
        return 0

    sqsend[...] = jnp.zeros_like(sqsend)
    weights = (0.5 / FD, 1.0 / FD, FD ** -0.5)

    def joined(ref, p):
        return jnp.concatenate([ref[p, c].reshape(outer_n * sub, head_dim) for c in range(2)], axis=0)

    def zrow_of(state, h):
        block = state[h * rows + LIN:h * rows + ONE + 8].astype(F32)
        return jnp.concatenate([block[ONE + 1 - LIN:ONE + 2 - LIN], block[ONE + 2 - LIN:ONE + 3 - LIN, :ONE + 8 - LANES]], axis=1)

    def outer(p):
        to_seq(fwd.at[p], pre.at[p, 1 - yi], s7.at[p], r7.at[p], mate).wait_recv()
        qt = qs[p].astype(F32).T
        state = joined(pre, p)
        live = (iota((span, 1), 0) + me * span < len_ref[p]).astype(F32)
        earlier = jnp.minimum(me * span, len_ref[p]).astype(F32)
        sq = jnp.zeros((sqsend.shape[0], span), F32)
        for h in range(heads):
            phi = features(qt[h * FD:(h + 1) * FD], rows, weights).astype(BF)
            zr = zrow_of(state, h)
            zr = jnp.where(iota(zr.shape, 1) == ONE, 0.0, zr)
            zb = jnp.broadcast_to(zr, (head_dim, zr.shape[1])).astype(BF)
            phit = phi.T
            num = dot(phit, state[h * rows:(h + 1) * rows]) + nd[p, h, :, :head_dim]
            den = dot(phit[:, :zr.shape[1]], zb, NT) + nd[p, h, :, head_dim:] + earlier
            att = num / den * live
            nd[p, h, :, :head_dim] = att
            sq = sq + dot(jnp.ones((sqsend.shape[0], head_dim), BF), (att * att).astype(BF), NT)
        sqsend[...] = jnp.where(iota(sq.shape, 0) == p, sq, sqsend[...])

    ztsend[...] = jnp.zeros_like(ztsend)
    per = FD * FD // nf
    pick = pick_matrix(0, FD * FD, rows).astype(BF)

    def spread(p):
        to_seq(tot.at[p, yi], tot.at[p, 1 - yi], s8.at[p], r8.at[p], mate).wait_recv()
        state = joined(tot, p)
        zt = ztsend[...]
        zrow = iota(zt.shape, 0)
        for h in range(heads):
            mine = state[h * rows:(h + 1) * rows]
            zr = zrow_of(state, h)
            zr = jnp.where(iota(zr.shape, 1) == ONE, len_ref[p].astype(F32), zr)
            zt = jnp.where(zrow == p * heads + h, zr, zt)
            full = dot(pick, mine).astype(BF)
            for f in range(nf):
                tsend[f, p, h] = full[f * per:(f + 1) * per]
            tail = mine[LIN:].astype(F32)
            low_out[p, h] = jnp.concatenate(
                [tail[ONE - LIN:ONE - LIN + 1], tail[:FD] * FD ** -0.25], axis=0)
        ztsend[...] = zt
        for i in range(1, nf):
            target = lax.rem(fi + i, nf)
            to_feat(tsend.at[target, p], quad_out.at[fi, p], s5.at[i, p], r5.at[fi, p], target).start()

    lax.fori_loop(0, npr // 2, inner, 0)
    pair_up(npr - 2)
    home(0)
    lax.fori_loop(npr // 2, npr, inner, 0)
    for p in range(1, npr - 2):
        home(p)
    for p in range(npr):
        if p == 0:
            pair_up(npr - 1)
        take_prefix(p)
        take_total(p)
        if p + npr - 2 < npr:
            home(p + npr - 2)
        if p > 0:
            outer(p - 1)
            spread(p - 1)
    outer(npr - 1)

    sqgot[fi] = sqsend[...]
    for i in range(1, nf):
        to_feat(sqsend, sqgot.at[fi], s4.at[i], r4.at[fi], lax.rem(fi + i, nf)).start()

    spread(npr - 1)
    zt = ztsend[...]
    ztgot[fi] = zt
    for i in range(1, nf):
        to_feat(ztsend, ztgot.at[fi], s6.at[i], r6.at[fi], lax.rem(fi + i, nf)).start()
    quad_out[fi] = tsend[fi]

    for i in range(1, nf):
        src = lax.rem(fi + i, nf)
        to_feat(sqsend, sqgot.at[src], s4.at[i], r4.at[src], fpeer).wait_recv()
    squares = sqgot[0]
    for f in range(1, nf):
        squares = squares + sqgot[f]
    width = nf * heads * head_dim
    mean = squares * (1.0 / width) + NORM_FLOOR
    inv = lax.rsqrt(mean)
    zsq = sqsend.shape[0]

    for p in range(npr):
        col = jnp.broadcast_to(inv[p:p + 1], (LANES, span)).T
        for h in range(heads):
            mixed[p, :, h * head_dim:(h + 1) * head_dim] = (nd[p, h, :, :head_dim] * col).astype(BF)

    for i in range(1, nf):
        src = lax.rem(fi + i, nf)
        to_feat(ztsend, ztgot.at[src], s6.at[i], r6.at[src], fpeer).wait_recv()
    own_pick = pick_matrix(fi * per, per, ONE + 8).astype(F32)
    for f in range(nf):
        nq = dot(ztgot[f], own_pick, NT, lax.Precision.HIGHEST) * (2.0 * FD) ** -0.5
        for p in range(npr):
            nq_out[p, f * heads:(f + 1) * heads] = nq[p * heads:(p + 1) * heads]
    lr, lc = iota((FD + 1, ONE + 8), 0), iota((FD + 1, ONE + 8), 1)
    low_pick = jnp.where(lr == 0, (lc == ONE).astype(F32), (lc == LIN - 1 + lr).astype(F32) * FD ** -0.25)
    nl = dot(ztgot[fi], low_pick, NT, lax.Precision.HIGHEST)
    for p in range(npr):
        nl_out[p] = nl[p * heads:(p + 1) * heads]

    for i in range(1, nf):
        src = lax.rem(fi + i, nf)

        @pl.loop(0, npr)
        def _(p):
            to_feat(tsend.at[src, p], quad_out.at[src, p], s5.at[i, p], r5.at[src, p], fpeer).wait_recv()
            to_feat(tsend.at[src, p], quad_out.at[src, p], s5.at[i, p], r5.at[src, p], fpeer).wait_send()
        to_feat(sqsend, sqgot.at[fi], s4.at[i], r4.at[fi], fpeer).wait_send()
        to_feat(ztsend, ztgot.at[fi], s6.at[i], r6.at[fi], fpeer).wait_send()

    @pl.loop(0, npr)
    def _(p):
        to_seq(part.at[p, yi], mgot.at[p], s0.at[p], r0.at[p], mate).wait_send()
        to_seq(fwd.at[p], pre.at[p, yi], s7.at[p], r7.at[p], mate).wait_send()
        to_seq(tot.at[p, yi], tot.at[p, yi], s8.at[p], r8.at[p], mate).wait_send()

        @pl.loop(1, outer_n)
        def _(i):
            there = lax.rem(zo + i, outer_n)
            to_seq(bsend.at[p, there], got.at[p, zo], s1.at[p, i], r1.at[p, zo], zpeer).wait_send()

            @pl.when(there != 0)
            def _():
                to_seq(presend.at[p, there], prer.at[p, zo], s2.at[p, i], r2.at[p, zo], zpeer).wait_send()

            @pl.when(there != last)
            def _():
                to_seq(tot.at[p, yi, zo], tot.at[p, yi, zo], s3.at[p, i], r3.at[p, zo], zpeer).wait_send()


def finish(cfg, own_ref, mixed, quad, low, nq, nl, mixed_out, quad_out, low_out, nq_out, nl_out):
    nf, heads = cfg
    p = pl.program_id(0)
    mask = (own_ref[p] == lax.axis_index("seq")).astype(F32)
    mixed_out[...] = mixed[...]
    for f in range(nf):
        quad_out[0, f * heads:(f + 1) * heads] = quad[f, 0].astype(F32) * (mask * (2.0 * FD) ** -0.5)
    for h in range(heads):
        low_out[0, :, h, :] = low[0, h] * mask
    nq_out[...] = nq[...] * mask
    nl_out[...] = nl[...] * mask


def body(hidden_in, w_query, w_key, w_value, lengths, owners):
    npr, span, width = hidden_in.shape
    n, nf = lax.axis_size("seq"), lax.axis_size("feat")
    heads = H // nf
    head_dim = width // H
    step = 16 * n // heads
    rows = -(-LIVE_ROWS // 8) * 8
    rows = -(-rows // step) * step
    sub = heads * rows // n
    cfg = (n, nf, npr, span, heads, rows, sub)
    per = FD * FD // nf
    dma = pltpu.SemaphoreType.DMA
    vm = pltpu.VMEM
    ph = npr * heads
    out = pl.pallas_call(
        functools.partial(kernel, cfg),
        out_shape=(
            jax.ShapeDtypeStruct((npr, span, heads * head_dim), BF),
            jax.ShapeDtypeStruct((nf, npr, heads, per, head_dim), BF),
            jax.ShapeDtypeStruct((npr, heads, FD + 1, head_dim), F32),
            jax.ShapeDtypeStruct((npr, H, per), F32),
            jax.ShapeDtypeStruct((npr, heads, FD + 1), F32),
        ),
        in_specs=[pl.BlockSpec(memory_space=pltpu.SMEM)] + [pl.BlockSpec(memory_space=pl.ANY)] * 4,
        out_specs=[pl.BlockSpec(memory_space=pltpu.VMEM)] * 5,
        scratch_shapes=[
            vm((npr, span, width), BF),
            vm((width, 2 * LANES), BF),
            vm((width, heads * head_dim), BF),
            vm((npr, span, heads * FD), BF),
            vm((npr, span, heads * FD), BF),
            vm((npr, span, heads * head_dim), BF),
            vm((npr, heads, span, 2 * head_dim), F32),
            vm((npr, 2, n // 2, sub, head_dim), BF),
            vm((npr, n // 2, sub, head_dim), BF),
            vm((npr, n // 2, sub, head_dim), BF),
            vm((npr, n // 2, sub, head_dim), BF),
            vm((npr, n // 2, sub, head_dim), BF),
            vm((npr, n // 2, sub, head_dim), BF),
            vm((npr, n // 2, sub, head_dim), BF),
            vm((npr, 2, n // 2, sub, head_dim), BF),
            vm((npr, 2, n // 2, sub, head_dim), BF),
            vm((nf, npr, heads, per, head_dim), BF),
            vm((8, span), F32),
            vm((nf, 8, span), F32),
            vm((ph, ONE + 8), F32),
            vm((nf, ph, ONE + 8), F32),
            dma((npr + 3,)),
            dma((npr,)), dma((npr,)), dma((npr, n // 2)), dma((npr, n // 2)),
            dma((npr, n // 2)), dma((npr, n // 2)), dma((npr, n // 2)), dma((npr, n // 2)),
            dma((nf,)), dma((nf,)), dma((nf, npr)), dma((nf, npr)), dma((nf,)), dma((nf,)),
            dma((npr,)), dma((npr,)), dma((npr,)), dma((npr,)),
        ],
        compiler_params=pltpu.CompilerParams(
            collective_id=0, has_side_effects=True, vmem_limit_bytes=56 * 1024 * 1024
        ),
        name="layer",
    )(lengths, hidden_in, w_query, w_key, w_value)
    mixed, quad, low, nq, nl = out
    block = pl.BlockSpec
    mixed, quad, low, nq, nl = pl.pallas_call(
        functools.partial(finish, (nf, heads)),
        grid=(npr,),
        out_shape=(
            jax.ShapeDtypeStruct(mixed.shape, BF),
            jax.ShapeDtypeStruct((npr, H, per, head_dim), F32),
            jax.ShapeDtypeStruct((npr, FD + 1, heads, head_dim), F32),
            jax.ShapeDtypeStruct(nq.shape, F32),
            jax.ShapeDtypeStruct(nl.shape, F32),
        ),
        in_specs=[
            block(memory_space=pltpu.SMEM),
            block((1, span, heads * head_dim), lambda p: (p, 0, 0)),
            block((nf, 1, heads, per, head_dim), lambda p: (0, p, 0, 0, 0)),
            block((1, heads, FD + 1, head_dim), lambda p: (p, 0, 0, 0)),
            block((1, H, per), lambda p: (p, 0, 0)),
            block((1, heads, FD + 1), lambda p: (p, 0, 0)),
        ],
        out_specs=[
            block((1, span, heads * head_dim), lambda p: (p, 0, 0)),
            block((1, H, per, head_dim), lambda p: (p, 0, 0, 0)),
            block((1, FD + 1, heads, head_dim), lambda p: (p, 0, 0, 0)),
            block((1, H, per), lambda p: (p, 0, 0)),
            block((1, heads, FD + 1), lambda p: (p, 0, 0)),
        ],
        name="finish",
    )(owners, mixed, quad, low, nq, nl)
    return (mixed, quad[None], jnp.transpose(low, (0, 2, 1, 3))[None], nq[None], nl[None])


def solution(mesh):
    placed = (P(None, "seq", None), P(), P(), P(None, "feat"), P(), P())
    return jax.shard_map(
        body,
        mesh=mesh,
        in_specs=placed,
        out_specs=(
            P(None, "seq", "feat"),
            P("seq", None, None, "feat", None),
            P("seq", None, "feat", None, None),
            P("seq", None, None, "feat"),
            P("seq", None, "feat", None),
        ),
        check_vma=False,
    )
```

time: 58.6 us -> 50.7 us (0.87)
  the two profiles are of different devices: /device:TPU:9 before, /device:TPU:0 now
where the time goes in v3:
time: 50.7 us; the launch traced here: 50.5 us
  Pallas kernels  49.9 us (98%)
  between operations  0.64 us (1%)
    pallas_call x1, Pallas kernels, body(): pl.pallas_call(functools.partial(kernel, cfg), out_shape=(jax.ShapeDtypeS...  45.9 us
    pallas_call x1, Pallas kernels, body(): pl.pallas_call(functools.partial(finish, (nf, heads)), grid=(npr,), out_s...  4.01 us

profile of v3, /device:TPU:0, one launch (start us, length us, event | category | flops | bytes accessed | tf_op | source)
XLA Modules:
  0.0 50.5 jit_solution(10441727794481326868)
XLA Ops:
  0.6 45.9 %layer.1 = (bf16[4,256,512]{2,1,0:T(8,128)(2,1)}, bf16[4,4,4,64,128]{4,3,2,1,0:T(8,128)(2,1)}, f32[4,4,17,128]{3,2,1,0:T(8,128)}, f32[4,16,64]{2,1,0:T(8,128)}, f32[4,4,17]{2,1,0:T(4,128)}) custom-call(s32[4]{0:T(128)} %len_ref.1, bf16[4,256,2048]{2,1,0:T(8,128)(2,1)} %x_hbm.1, bf16[2048,256]{1,0:T(8,128)(2,1)} %wq_hbm.1, bf16[2048,256]{1,0:T(8,128)(2,1)} %wk_hbm.1, ...), custom_call_target="tpu_custom_call" | custom-call | tf_op jit(solution)/shard_map/layer/pallas_call | solution.py:413
  46.5 4.0 %finish.1 = (bf16[4,256,512]{2,1,0:T(8,128)(2,1)}, f32[4,16,64,128]{3,2,1,0:T(8,128)}, f32[4,17,4,128]{3,2,1,0:T(4,128)}, f32[4,16,64]{2,1,0:T(8,128)}, f32[4,4,17]{2,1,0:T(4,128)}) custom-call(s32[4]{0:T(128)} %own_ref.1, bf16[4,256,512]{2,1,0:T(8,128)(2,1)} %get-tuple-element.15.mixed, bf16[4,4,4,64,128]{4,3,2,1,0:T(8,128)(2,1)} %get-tuple-element.16.quad, ...), custom_call_target="tpu_custom_call" | custom-call | tf_op jit(solution)/shard_map/finish/pallas_call | solution.py:459

commit v4 on v3

--- a/solution.py
+++ b/solution.py
@@ -150,9 +150,9 @@
             part[p, c] = jnp.concatenate(sums[c * half:(c + 1) * half], axis=0).reshape(outer_n, sub, head_dim)
         to_seq(part.at[p, 1 - yi], mgot.at[p], s0.at[p], r0.at[p], mate).start()
 
-        @pl.when(p > 1)
+        @pl.when(p > 0)
         def _():
-            pair_up(p - 2)
+            pair_up(p - 1)
         return 0
 
     def pair_up(p):
@@ -295,7 +295,6 @@
             to_feat(tsend.at[target, p], quad_out.at[fi, p], s5.at[i, p], r5.at[fi, p], target).start()
 
     lax.fori_loop(0, npr // 2, inner, 0)
-    pair_up(npr - 2)
     home(0)
     lax.fori_loop(npr // 2, npr, inner, 0)
     for p in range(1, npr - 2):
@@ -385,15 +384,20 @@
 
 def finish(cfg, own_ref, mixed, quad, low, nq, nl, mixed_out, quad_out, low_out, nq_out, nl_out):
     nf, heads = cfg
-    p = pl.program_id(0)
-    mask = (own_ref[p] == lax.axis_index("seq")).astype(F32)
     mixed_out[...] = mixed[...]
+    count = nq.shape[0]
+    for b in range(count):
+        mask = (own_ref[pl.program_id(0) * count + b] == lax.axis_index("seq")).astype(F32)
+        finish_one(nf, heads, b, mask, quad, low, nq, nl, quad_out, low_out, nq_out, nl_out)
+
+
+def finish_one(nf, heads, b, mask, quad, low, nq, nl, quad_out, low_out, nq_out, nl_out):
     for f in range(nf):
-        quad_out[0, f * heads:(f + 1) * heads] = quad[f, 0].astype(F32) * (mask * (2.0 * FD) ** -0.5)
+        quad_out[b, f * heads:(f + 1) * heads] = quad[f, b].astype(F32) * (mask * (2.0 * FD) ** -0.5)
     for h in range(heads):
-        low_out[0, :, h, :] = low[0, h] * mask
-    nq_out[...] = nq[...] * mask
-    nl_out[...] = nl[...] * mask
+        low_out[b, :, h, :] = low[b, h] * mask
+    nq_out[b] = nq[b] * mask
+    nl_out[b] = nl[b] * mask
 
 
 def body(hidden_in, w_query, w_key, w_value, lengths, owners):
@@ -456,9 +460,10 @@
     )(lengths, hidden_in, w_query, w_key, w_value)
     mixed, quad, low, nq, nl = out
     block = pl.BlockSpec
+    group = 2 - npr % 2
     mixed, quad, low, nq, nl = pl.pallas_call(
         functools.partial(finish, (nf, heads)),
-        grid=(npr,),
+        grid=(npr // group,),
         out_shape=(
             jax.ShapeDtypeStruct(mixed.shape, BF),
             jax.ShapeDtypeStruct((npr, H, per, head_dim), F32),
@@ -468,18 +473,18 @@
         ),
         in_specs=[
             block(memory_space=pltpu.SMEM),
-            block((1, span, heads * head_dim), lambda p: (p, 0, 0)),
-            block((nf, 1, heads, per, head_dim), lambda p: (0, p, 0, 0, 0)),
-            block((1, heads, FD + 1, head_dim), lambda p: (p, 0, 0, 0)),
-            block((1, H, per), lambda p: (p, 0, 0)),
-            block((1, heads, FD + 1), lambda p: (p, 0, 0)),
+            block((group, span, heads * head_dim), lambda p: (p, 0, 0)),
+            block((nf, group, heads, per, head_dim), lambda p: (0, p, 0, 0, 0)),
+            block((group, heads, FD + 1, head_dim), lambda p: (p, 0, 0, 0)),
+            block((group, H, per), lambda p: (p, 0, 0)),
+            block((group, heads, FD + 1), lambda p: (p, 0, 0)),
         ],
         out_specs=[
-            block((1, span, heads * head_dim), lambda p: (p, 0, 0)),
-            block((1, H, per, head_dim), lambda p: (p, 0, 0, 0)),
-            block((1, FD + 1, heads, head_dim), lambda p: (p, 0, 0, 0)),
-            block((1, H, per), lambda p: (p, 0, 0)),
-            block((1, heads, FD + 1), lambda p: (p, 0, 0)),
+            block((group, span, heads * head_dim), lambda p: (p, 0, 0)),
+            block((group, H, per, head_dim), lambda p: (p, 0, 0, 0)),
+            block((group, FD + 1, heads, head_dim), lambda p: (p, 0, 0, 0)),
+            block((group, H, per), lambda p: (p, 0, 0)),
+            block((group, heads, FD + 1), lambda p: (p, 0, 0)),
         ],
         name="finish",
     )(owners, mixed, quad, low, nq, nl)

time: 50.7 us -> 49.5 us (0.976)
  Pallas kernels: 49.9 us -> 48.7 us
    pallas_call x1, Pallas kernels: 4.01 us -> 3.07 us  [body(): pl.pallas_call(functools.partial(finish, (nf, heads)), grid=(npr // group...]
where the time goes in v4:
time: 49.5 us; the launch traced here: 49.4 us
  Pallas kernels  48.7 us (98%)
  between operations  0.64 us (1%)
    pallas_call x1, Pallas kernels, body(): pl.pallas_call(functools.partial(kernel, cfg), out_shape=(jax.ShapeDtypeS...  45.6 us
    pallas_call x1, Pallas kernels, body(): pl.pallas_call(functools.partial(finish, (nf, heads)), grid=(npr // group...  3.07 us

profile of v4, /device:TPU:0, one launch (start us, length us, event | category | flops | bytes accessed | tf_op | source)
XLA Modules:
  0.0 49.4 jit_solution(2440701114116534388)
XLA Ops:
  0.6 45.6 %layer.1 = (bf16[4,256,512]{2,1,0:T(8,128)(2,1)}, bf16[4,4,4,64,128]{4,3,2,1,0:T(8,128)(2,1)}, f32[4,4,17,128]{3,2,1,0:T(8,128)}, f32[4,16,64]{2,1,0:T(8,128)}, f32[4,4,17]{2,1,0:T(4,128)}) custom-call(s32[4]{0:T(128)} %len_ref.1, bf16[4,256,2048]{2,1,0:T(8,128)(2,1)} %x_hbm.1, bf16[2048,256]{1,0:T(8,128)(2,1)} %wq_hbm.1, bf16[2048,256]{1,0:T(8,128)(2,1)} %wk_hbm.1, ...), custom_call_target="tpu_custom_call" | custom-call | tf_op jit(solution)/shard_map/layer/pallas_call | solution.py:417
  46.3 3.1 %finish.1 = (bf16[4,256,512]{2,1,0:T(8,128)(2,1)}, f32[4,16,64,128]{3,2,1,0:T(8,128)}, f32[4,17,4,128]{3,2,1,0:T(4,128)}, f32[4,16,64]{2,1,0:T(8,128)}, f32[4,4,17]{2,1,0:T(4,128)}) custom-call(s32[4]{0:T(128)} %own_ref.1, bf16[4,256,512]{2,1,0:T(8,128)(2,1)} %get-tuple-element.15.mixed, bf16[4,4,4,64,128]{4,3,2,1,0:T(8,128)(2,1)} %get-tuple-element.16.quad, ...), custom_call_target="tpu_custom_call" | custom-call | tf_op jit(solution)/shard_map/finish/pallas_call | solution.py:464
